TPU v7x, 32 devices: a whole 2x2x4 slice. The times are simulated.
32 devices in a mesh: pb: 4 (over x, core), kv: 8 (over z, y).
Axes of the slice: x: 2, y: 2, z: 4, core: 2. Of those that a mesh axis runs over, the one named last changes fastest.
Arguments:
- queries: bfloat16 [32768, 256], P(('pb', 'kv')), may hold values from -64 to 64
- keys: bfloat16 [1024, 256], P('kv'), may hold values from -6 to 6
- values: bfloat16 [1024, 256], P('kv'), may hold values from -6 to 6
- dout: bfloat16 [32768, 256], P(('pb', 'kv')), may hold values from -256 to 256
Outputs:
- dq: float32 [32768, 256], P(('pb', 'kv'))
- dk: float32 [1024, 256], P('kv')
- dv: float32 [1024, 256], P('kv')
All inputs are finite; a program needn't handle non-finite values.
Results may differ from a plain program's by a relative error of at most 0.0029.
Values may be sent and summed in bfloat16 or wider, within the bound.
No kernel may reach another device: no remote copies, remote signals or barrier semaphores. Data moves between devices by JAX's collectives and lax.ppermute only.
A program may use at most 64 MiB of HBM per device.

v0:
```python
import math
import jax
import jax.numpy as jnp
from jax import lax
from jax.sharding import PartitionSpec as P

H = 2
DH = 128


def from_behind(value, axis, by):
    peers = lax.axis_size(axis)
    return lax.ppermute(value, axis, [(i, (i + by) % peers) for i in range(peers)])


def split_heads(matrix):
    return matrix.reshape(matrix.shape[0], H, DH)


def block_scores(query_blk, grad_blk, key_blk, value_blk):
    score_scale = 1.0 / math.sqrt(DH)
    logits = (
        jnp.einsum("qhd,khd->hqk", query_blk, key_blk, preferred_element_type=jnp.float32)
        * score_scale
    )
    dprob = jnp.einsum("qhd,khd->hqk", grad_blk, value_blk, preferred_element_type=jnp.float32)
    return (logits, dprob)


def empty_stats(row_count):
    return (
        jnp.full((H, row_count), -1e30, jnp.float32),
        jnp.zeros((H, row_count), jnp.float32),
        jnp.zeros((H, row_count), jnp.float32),
    )


def fold_stats(totals, logits, dprob):
    peak, mass, weighted = totals
    new_peak = jnp.maximum(peak, jnp.max(logits, axis=-1))
    keep = jnp.exp(peak - new_peak)
    shifted = jnp.exp(logits - new_peak[..., None])
    return (
        new_peak,
        mass * keep + jnp.sum(shifted, axis=-1),
        weighted * keep + jnp.sum(shifted * dprob, axis=-1),
    )


def block_grads(query_blk, grad_blk, key_blk, value_blk, lse, delta):
    score_scale = 1.0 / math.sqrt(DH)
    logits, dprob = block_scores(query_blk, grad_blk, key_blk, value_blk)
    probs = jnp.exp(logits - lse[..., None])
    dlogits = probs * (dprob - delta[..., None])
    probs_b = probs.astype(jnp.bfloat16)
    dlogits_b = dlogits.astype(jnp.bfloat16)
    dv_part = jnp.einsum("hqk,qhd->khd", probs_b, grad_blk, preferred_element_type=jnp.float32)
    dk_part = (
        jnp.einsum("hqk,qhd->khd", dlogits_b, query_blk, preferred_element_type=jnp.float32)
        * score_scale
    )
    dq_part = (
        jnp.einsum("hqk,khd->qhd", dlogits_b, key_blk, preferred_element_type=jnp.float32)
        * score_scale
    )
    return (dq_part, dk_part, dv_part)


def local(queries, keys, values, dout):
    cycle_size = lax.axis_size("kv")
    query_rows = queries.shape[0]
    key_rows = keys.shape[0]
    query_heads = split_heads(queries)
    grad_heads = split_heads(dout)
    key_vals = jnp.stack([split_heads(keys), split_heads(values)])

    def stat_step(step_index, carry):
        moving, totals = carry
        logits, dprob = block_scores(query_heads, grad_heads, moving[0], moving[1])
        totals = fold_stats(totals, logits, dprob)
        moving = from_behind(moving, "kv", 1)
        return (moving, totals)

    key_vals, totals = lax.fori_loop(0, cycle_size, stat_step, (key_vals, empty_stats(query_rows)))
    lse = totals[0] + jnp.log(totals[1])
    delta = totals[2] / totals[1]

    def grad_step(step_index, carry):
        moving, grads_acc, dq_acc = carry
        dq_part, dk_part, dv_part = block_grads(
            query_heads, grad_heads, moving[0], moving[1], lse, delta
        )
        grads_acc = grads_acc + jnp.stack([dk_part, dv_part])
        moving = from_behind(moving, "kv", 1)
        grads_acc = from_behind(grads_acc, "kv", 1)
        return (moving, grads_acc, dq_acc + dq_part)

    start = (
        key_vals,
        jnp.zeros((2, key_rows, H, DH), jnp.float32),
        jnp.zeros((query_rows, H, DH), jnp.float32),
    )
    key_vals, grads_acc, dq_acc = lax.fori_loop(0, cycle_size, grad_step, start)
    dq = dq_acc.reshape(query_rows, H * DH)
    summed = lax.psum(grads_acc, "pb")
    return (dq, summed[0].reshape(key_rows, H * DH), summed[1].reshape(key_rows, H * DH))


def solution(mesh):
    return jax.shard_map(
        local,
        mesh=mesh,
        in_specs=(P(("pb", "kv"), None), P("kv", None), P("kv", None), P(("pb", "kv"), None)),
        out_specs=(P(("pb", "kv"), None), P("kv", None), P("kv", None)),
        check_vma=False,
    )
```

profile of v0, /device:TPU:0, one launch (start us, length us, event | category | flops | bytes accessed | tf_op | source)
XLA Modules:
  0.0 225.6 jit_solution(1667497110011160057)
XLA Ops:
  7.2 1.2 copy.16
  8.8 0.8 copy-done.1
  11.7 66.0 %while.32 = (s32[]{:T(128)}, bf16[2,128,2,128]{3,1,2,0:T(8,128)(2,1)S(1)}, f32[2,1024]{1,0:T(2,128)S(1)}, f32[2,1024]{1,0:T(2,128)S(1)}, f32[2,1024]{1,0:T(2,128...) while((s32[]{:T(128)}, ...), condition=%wide.region_4.0_spmd.clone, body=%wide.region_0.0_spmd.clone.sunk | while | flops 136067072 | bytes 5259408 | solution.py:84
  11.7 3.0 %collective-permute-start = (bf16[2,128,2,128]{3,1,2,0:T(8,128)(2,1)S(1)}, bf16[2,128,2,128]{3,1,2,0:T(8,128)(2,1)S(1)}, u32[]{:S(2)}, u32[]{:S(2)}) collective-permute-start(bf16[2,128,2,128]{3,1,2,0:T(8,128)(2,1)S(1)} %copy.40), channel_id=1, source_target_pairs={{0,1},{1,2},{2,3},{3,4},{4,5},{5,6},{6,7},{7,0},{8,9},{9,10},{10,1... | collective-permute-start | bytes 393224 | tf_op jit(solution)/shard_map/while/body/eval_jaxpr/ppermute | solution.py:13
  15.7 5.7 %collective-permute-done = bf16[2,128,2,128]{3,1,2,0:T(8,128)(2,1)S(1)} collective-permute-done((bf16[2,128,2,128]{3,1,2,0:T(8,128)(2,1)S(1)}, bf16[2,128,2,128]{3,1,2,0:T(8,128)(2,1)S(1)}, u32[]{:S(2)}, u32[]{:S(2)}) %collective-permute-start) | collective-permute-done | bytes 131104 | tf_op jit(solution)/shard_map/while/body/eval_jaxpr/ppermute | solution.py:13
  22.3 6.8 %collective-permute-done = bf16[2,128,2,128]{3,1,2,0:T(8,128)(2,1)S(1)} collective-permute-done((bf16[2,128,2,128]{3,1,2,0:T(8,128)(2,1)S(1)}, bf16[2,128,2,128]{3,1,2,0:T(8,128)(2,1)S(1)}, u32[]{:S(2)}, u32[]{:S(2)}) %collective-permute-start) | collective-permute-done | bytes 131104 | tf_op jit(solution)/shard_map/while/body/eval_jaxpr/ppermute | solution.py:13
  30.0 6.8 %collective-permute-done = bf16[2,128,2,128]{3,1,2,0:T(8,128)(2,1)S(1)} collective-permute-done((bf16[2,128,2,128]{3,1,2,0:T(8,128)(2,1)S(1)}, bf16[2,128,2,128]{3,1,2,0:T(8,128)(2,1)S(1)}, u32[]{:S(2)}, u32[]{:S(2)}) %collective-permute-start) | collective-permute-done | bytes 131104 | tf_op jit(solution)/shard_map/while/body/eval_jaxpr/ppermute | solution.py:13
  37.8 6.8 %collective-permute-done = bf16[2,128,2,128]{3,1,2,0:T(8,128)(2,1)S(1)} collective-permute-done((bf16[2,128,2,128]{3,1,2,0:T(8,128)(2,1)S(1)}, bf16[2,128,2,128]{3,1,2,0:T(8,128)(2,1)S(1)}, u32[]{:S(2)}, u32[]{:S(2)}) %collective-permute-start) | collective-permute-done | bytes 131104 | tf_op jit(solution)/shard_map/while/body/eval_jaxpr/ppermute | solution.py:13
  45.5 6.8 %collective-permute-done = bf16[2,128,2,128]{3,1,2,0:T(8,128)(2,1)S(1)} collective-permute-done((bf16[2,128,2,128]{3,1,2,0:T(8,128)(2,1)S(1)}, bf16[2,128,2,128]{3,1,2,0:T(8,128)(2,1)S(1)}, u32[]{:S(2)}, u32[]{:S(2)}) %collective-permute-start) | collective-permute-done | bytes 131104 | tf_op jit(solution)/shard_map/while/body/eval_jaxpr/ppermute | solution.py:13
  53.2 7.9 %collective-permute-done = bf16[2,128,2,128]{3,1,2,0:T(8,128)(2,1)S(1)} collective-permute-done((bf16[2,128,2,128]{3,1,2,0:T(8,128)(2,1)S(1)}, bf16[2,128,2,128]{3,1,2,0:T(8,128)(2,1)S(1)}, u32[]{:S(2)}, u32[]{:S(2)}) %collective-permute-start) | collective-permute-done | bytes 131104 | tf_op jit(solution)/shard_map/while/body/eval_jaxpr/ppermute | solution.py:13
  62.1 7.3 %collective-permute-done = bf16[2,128,2,128]{3,1,2,0:T(8,128)(2,1)S(1)} collective-permute-done((bf16[2,128,2,128]{3,1,2,0:T(8,128)(2,1)S(1)}, bf16[2,128,2,128]{3,1,2,0:T(8,128)(2,1)S(1)}, u32[]{:S(2)}, u32[]{:S(2)}) %collective-permute-start) | collective-permute-done | bytes 131104 | tf_op jit(solution)/shard_map/while/body/eval_jaxpr/ppermute | solution.py:13
  70.4 7.4 %collective-permute-done = bf16[2,128,2,128]{3,1,2,0:T(8,128)(2,1)S(1)} collective-permute-done((bf16[2,128,2,128]{3,1,2,0:T(8,128)(2,1)S(1)}, bf16[2,128,2,128]{3,1,2,0:T(8,128)(2,1)S(1)}, u32[]{:S(2)}, u32[]{:S(2)}) %collective-permute-start) | collective-permute-done | bytes 131104 | tf_op jit(solution)/shard_map/while/body/eval_jaxpr/ppermute | solution.py:13
  77.8 106.9 %while.33 = (s32[]{:T(128)}, bf16[2,128,2,128]{3,1,2,0:T(8,128)(2,1)S(1)}, f32[2,128,2,128]{3,1,2,0:T(8,128)S(1)}, f32[1024,2,128]{2,0,1:T(8,128)S(1)}, bf16[102...) while((s32[]{:T(128)}, ...), condition=%wide.region_6.0_spmd.clone, body=%wide.region_5.0_spmd.clone.sunk | while | flops 338067456 | bytes 12009663 | solution.py:103
  80.5 5.5 %collective-permute-done.1 = bf16[2,128,2,128]{3,1,2,0:T(8,128)(2,1)S(1)} collective-permute-done((bf16[2,128,2,128]{3,1,2,0:T(8,128)(2,1)S(1)}, bf16[2,128,2,128]{3,1,2,0:T(8,128)(2,1)S(1)}, u32[]{:S(2)}, u32[]{:S(2)}) %collective-permute-start.1) | collective-permute-done | bytes 131104 | tf_op jit(solution)/shard_map/while/body/eval_jaxpr/ppermute | solution.py:13
  86.0 6.0 %collective-permute-done.2 = f32[2,128,2,128]{3,1,2,0:T(8,128)S(1)} collective-permute-done((f32[2,128,2,128]{3,1,2,0:T(8,128)}, f32[2,128,2,128]{3,1,2,0:T(8,128)S(1)}, u32[]{:S(2)}, u32[]{:S(2)}) %collective-permute-start.2) | collective-permute-done | bytes 262176 | tf_op jit(solution)/shard_map/while/body/eval_jaxpr/ppermute | solution.py:13
  94.7 6.2 %collective-permute-done.1 = bf16[2,128,2,128]{3,1,2,0:T(8,128)(2,1)S(1)} collective-permute-done((bf16[2,128,2,128]{3,1,2,0:T(8,128)(2,1)S(1)}, bf16[2,128,2,128]{3,1,2,0:T(8,128)(2,1)S(1)}, u32[]{:S(2)}, u32[]{:S(2)}) %collective-permute-start.1) | collective-permute-done | bytes 131104 | tf_op jit(solution)/shard_map/while/body/eval_jaxpr/ppermute | solution.py:13
  100.9 5.2 %collective-permute-done.2 = f32[2,128,2,128]{3,1,2,0:T(8,128)S(1)} collective-permute-done((f32[2,128,2,128]{3,1,2,0:T(8,128)}, f32[2,128,2,128]{3,1,2,0:T(8,128)S(1)}, u32[]{:S(2)}, u32[]{:S(2)}) %collective-permute-start.2) | collective-permute-done | bytes 262176 | tf_op jit(solution)/shard_map/while/body/eval_jaxpr/ppermute | solution.py:13
  108.9 5.6 %collective-permute-done.1 = bf16[2,128,2,128]{3,1,2,0:T(8,128)(2,1)S(1)} collective-permute-done((bf16[2,128,2,128]{3,1,2,0:T(8,128)(2,1)S(1)}, bf16[2,128,2,128]{3,1,2,0:T(8,128)(2,1)S(1)}, u32[]{:S(2)}, u32[]{:S(2)}) %collective-permute-start.1) | collective-permute-done | bytes 131104 | tf_op jit(solution)/shard_map/while/body/eval_jaxpr/ppermute | solution.py:13
  114.4 5.2 %collective-permute-done.2 = f32[2,128,2,128]{3,1,2,0:T(8,128)S(1)} collective-permute-done((f32[2,128,2,128]{3,1,2,0:T(8,128)}, f32[2,128,2,128]{3,1,2,0:T(8,128)S(1)}, u32[]{:S(2)}, u32[]{:S(2)}) %collective-permute-start.2) | collective-permute-done | bytes 262176 | tf_op jit(solution)/shard_map/while/body/eval_jaxpr/ppermute | solution.py:13
  122.4 5.7 %collective-permute-done.1 = bf16[2,128,2,128]{3,1,2,0:T(8,128)(2,1)S(1)} collective-permute-done((bf16[2,128,2,128]{3,1,2,0:T(8,128)(2,1)S(1)}, bf16[2,128,2,128]{3,1,2,0:T(8,128)(2,1)S(1)}, u32[]{:S(2)}, u32[]{:S(2)}) %collective-permute-start.1) | collective-permute-done | bytes 131104 | tf_op jit(solution)/shard_map/while/body/eval_jaxpr/ppermute | solution.py:13
  128.1 4.9 %collective-permute-done.2 = f32[2,128,2,128]{3,1,2,0:T(8,128)S(1)} collective-permute-done((f32[2,128,2,128]{3,1,2,0:T(8,128)}, f32[2,128,2,128]{3,1,2,0:T(8,128)S(1)}, u32[]{:S(2)}, u32[]{:S(2)}) %collective-permute-start.2) | collective-permute-done | bytes 262176 | tf_op jit(solution)/shard_map/while/body/eval_jaxpr/ppermute | solution.py:13
  135.7 5.9 %collective-permute-done.1 = bf16[2,128,2,128]{3,1,2,0:T(8,128)(2,1)S(1)} collective-permute-done((bf16[2,128,2,128]{3,1,2,0:T(8,128)(2,1)S(1)}, bf16[2,128,2,128]{3,1,2,0:T(8,128)(2,1)S(1)}, u32[]{:S(2)}, u32[]{:S(2)}) %collective-permute-start.1) | collective-permute-done | bytes 131104 | tf_op jit(solution)/shard_map/while/body/eval_jaxpr/ppermute | solution.py:13
  141.6 4.8 %collective-permute-done.2 = f32[2,128,2,128]{3,1,2,0:T(8,128)S(1)} collective-permute-done((f32[2,128,2,128]{3,1,2,0:T(8,128)}, f32[2,128,2,128]{3,1,2,0:T(8,128)S(1)}, u32[]{:S(2)}, u32[]{:S(2)}) %collective-permute-start.2) | collective-permute-done | bytes 262176 | tf_op jit(solution)/shard_map/while/body/eval_jaxpr/ppermute | solution.py:13
  149.1 5.9 %collective-permute-done.1 = bf16[2,128,2,128]{3,1,2,0:T(8,128)(2,1)S(1)} collective-permute-done((bf16[2,128,2,128]{3,1,2,0:T(8,128)(2,1)S(1)}, bf16[2,128,2,128]{3,1,2,0:T(8,128)(2,1)S(1)}, u32[]{:S(2)}, u32[]{:S(2)}) %collective-permute-start.1) | collective-permute-done | bytes 131104 | tf_op jit(solution)/shard_map/while/body/eval_jaxpr/ppermute | solution.py:13
  155.0 4.8 %collective-permute-done.2 = f32[2,128,2,128]{3,1,2,0:T(8,128)S(1)} collective-permute-done((f32[2,128,2,128]{3,1,2,0:T(8,128)}, f32[2,128,2,128]{3,1,2,0:T(8,128)S(1)}, u32[]{:S(2)}, u32[]{:S(2)}) %collective-permute-start.2) | collective-permute-done | bytes 262176 | tf_op jit(solution)/shard_map/while/body/eval_jaxpr/ppermute | solution.py:13
  162.4 5.9 %collective-permute-done.1 = bf16[2,128,2,128]{3,1,2,0:T(8,128)(2,1)S(1)} collective-permute-done((bf16[2,128,2,128]{3,1,2,0:T(8,128)(2,1)S(1)}, bf16[2,128,2,128]{3,1,2,0:T(8,128)(2,1)S(1)}, u32[]{:S(2)}, u32[]{:S(2)}) %collective-permute-start.1) | collective-permute-done | bytes 131104 | tf_op jit(solution)/shard_map/while/body/eval_jaxpr/ppermute | solution.py:13
  168.3 4.8 %collective-permute-done.2 = f32[2,128,2,128]{3,1,2,0:T(8,128)S(1)} collective-permute-done((f32[2,128,2,128]{3,1,2,0:T(8,128)}, f32[2,128,2,128]{3,1,2,0:T(8,128)S(1)}, u32[]{:S(2)}, u32[]{:S(2)}) %collective-permute-start.2) | collective-permute-done | bytes 262176 | tf_op jit(solution)/shard_map/while/body/eval_jaxpr/ppermute | solution.py:13
  175.8 5.0 %collective-permute-done.1 = bf16[2,128,2,128]{3,1,2,0:T(8,128)(2,1)S(1)} collective-permute-done((bf16[2,128,2,128]{3,1,2,0:T(8,128)(2,1)S(1)}, bf16[2,128,2,128]{3,1,2,0:T(8,128)(2,1)S(1)}, u32[]{:S(2)}, u32[]{:S(2)}) %collective-permute-start.1) | collective-permute-done | bytes 131104 | tf_op jit(solution)/shard_map/while/body/eval_jaxpr/ppermute | solution.py:13
  180.8 3.8 %collective-permute-done.2 = f32[2,128,2,128]{3,1,2,0:T(8,128)S(1)} collective-permute-done((f32[2,128,2,128]{3,1,2,0:T(8,128)}, f32[2,128,2,128]{3,1,2,0:T(8,128)S(1)}, u32[]{:S(2)}, u32[]{:S(2)}) %collective-permute-start.2) | collective-permute-done | bytes 262176 | tf_op jit(solution)/shard_map/while/body/eval_jaxpr/ppermute | solution.py:13
  185.4 1.1 copy_bitcast_fusion
  186.4 30.3 %all-reduce.2.cloned.1.call-done = f32[2,128,2,128]{3,1,2,0:T(8,128)} async-done(((f32[2,128,2,128]{3,1,2,0:T(8,128)}), f32[2,128,2,128]{3,1,2,0:T(8,128)}) %all-reduce.2.cloned.1.call-update) | async-done | bytes 262160 | tf_op jit(solution)/shard_map/psum | solution.py:105
  216.8 1.0 fusion.24
  (160 shorter events, 32.7 us)
Async XLA Ops:
  7.2 209.6 %all-reduce.2.cloned.1.call-start = ((), (), s32[]{:S(2)}) async-start(), calls=%async_computation | async-start | bytes 524288 | tf_op jit(solution)/shard_map/psum | solution.py:105
  8.5 1.0 copy-start.1
  9.8 0.8 copy-start.2
  10.6 0.8 copy-start.3
  11.7 9.6 %collective-permute-start = (bf16[2,128,2,128]{3,1,2,0:T(8,128)(2,1)S(1)}, bf16[2,128,2,128]{3,1,2,0:T(8,128)(2,1)S(1)}, u32[]{:S(2)}, u32[]{:S(2)}) collective-permute-start(bf16[2,128,2,128]{3,1,2,0:T(8,128)(2,1)S(1)} %copy.40), channel_id=1, source_target_pairs={{0,1},{1,2},{2,3},{3,4},{4,5},{5,6},{6,7},{7,0},{8,9},{9,10},{10,1... | collective-permute-start | bytes 393224 | tf_op jit(solution)/shard_map/while/body/eval_jaxpr/ppermute | solution.py:13
  21.3 7.7 %collective-permute-start = (bf16[2,128,2,128]{3,1,2,0:T(8,128)(2,1)S(1)}, bf16[2,128,2,128]{3,1,2,0:T(8,128)(2,1)S(1)}, u32[]{:S(2)}, u32[]{:S(2)}) collective-permute-start(bf16[2,128,2,128]{3,1,2,0:T(8,128)(2,1)S(1)} %copy.40), channel_id=1, source_target_pairs={{0,1},{1,2},{2,3},{3,4},{4,5},{5,6},{6,7},{7,0},{8,9},{9,10},{10,1... | collective-permute-start | bytes 393224 | tf_op jit(solution)/shard_map/while/body/eval_jaxpr/ppermute | solution.py:13
  29.1 7.7 %collective-permute-start = (bf16[2,128,2,128]{3,1,2,0:T(8,128)(2,1)S(1)}, bf16[2,128,2,128]{3,1,2,0:T(8,128)(2,1)S(1)}, u32[]{:S(2)}, u32[]{:S(2)}) collective-permute-start(bf16[2,128,2,128]{3,1,2,0:T(8,128)(2,1)S(1)} %copy.40), channel_id=1, source_target_pairs={{0,1},{1,2},{2,3},{3,4},{4,5},{5,6},{6,7},{7,0},{8,9},{9,10},{10,1... | collective-permute-start | bytes 393224 | tf_op jit(solution)/shard_map/while/body/eval_jaxpr/ppermute | solution.py:13
  36.8 7.7 %collective-permute-start = (bf16[2,128,2,128]{3,1,2,0:T(8,128)(2,1)S(1)}, bf16[2,128,2,128]{3,1,2,0:T(8,128)(2,1)S(1)}, u32[]{:S(2)}, u32[]{:S(2)}) collective-permute-start(bf16[2,128,2,128]{3,1,2,0:T(8,128)(2,1)S(1)} %copy.40), channel_id=1, source_target_pairs={{0,1},{1,2},{2,3},{3,4},{4,5},{5,6},{6,7},{7,0},{8,9},{9,10},{10,1... | collective-permute-start | bytes 393224 | tf_op jit(solution)/shard_map/while/body/eval_jaxpr/ppermute | solution.py:13
  44.5 7.7 %collective-permute-start = (bf16[2,128,2,128]{3,1,2,0:T(8,128)(2,1)S(1)}, bf16[2,128,2,128]{3,1,2,0:T(8,128)(2,1)S(1)}, u32[]{:S(2)}, u32[]{:S(2)}) collective-permute-start(bf16[2,128,2,128]{3,1,2,0:T(8,128)(2,1)S(1)} %copy.40), channel_id=1, source_target_pairs={{0,1},{1,2},{2,3},{3,4},{4,5},{5,6},{6,7},{7,0},{8,9},{9,10},{10,1... | collective-permute-start | bytes 393224 | tf_op jit(solution)/shard_map/while/body/eval_jaxpr/ppermute | solution.py:13
  52.3 8.8 %collective-permute-start = (bf16[2,128,2,128]{3,1,2,0:T(8,128)(2,1)S(1)}, bf16[2,128,2,128]{3,1,2,0:T(8,128)(2,1)S(1)}, u32[]{:S(2)}, u32[]{:S(2)}) collective-permute-start(bf16[2,128,2,128]{3,1,2,0:T(8,128)(2,1)S(1)} %copy.40), channel_id=1, source_target_pairs={{0,1},{1,2},{2,3},{3,4},{4,5},{5,6},{6,7},{7,0},{8,9},{9,10},{10,1... | collective-permute-start | bytes 393224 | tf_op jit(solution)/shard_map/while/body/eval_jaxpr/ppermute | solution.py:13
  61.1 8.3 %collective-permute-start = (bf16[2,128,2,128]{3,1,2,0:T(8,128)(2,1)S(1)}, bf16[2,128,2,128]{3,1,2,0:T(8,128)(2,1)S(1)}, u32[]{:S(2)}, u32[]{:S(2)}) collective-permute-start(bf16[2,128,2,128]{3,1,2,0:T(8,128)(2,1)S(1)} %copy.40), channel_id=1, source_target_pairs={{0,1},{1,2},{2,3},{3,4},{4,5},{5,6},{6,7},{7,0},{8,9},{9,10},{10,1... | collective-permute-start | bytes 393224 | tf_op jit(solution)/shard_map/while/body/eval_jaxpr/ppermute | solution.py:13
  69.4 8.3 %collective-permute-start = (bf16[2,128,2,128]{3,1,2,0:T(8,128)(2,1)S(1)}, bf16[2,128,2,128]{3,1,2,0:T(8,128)(2,1)S(1)}, u32[]{:S(2)}, u32[]{:S(2)}) collective-permute-start(bf16[2,128,2,128]{3,1,2,0:T(8,128)(2,1)S(1)} %copy.40), channel_id=1, source_target_pairs={{0,1},{1,2},{2,3},{3,4},{4,5},{5,6},{6,7},{7,0},{8,9},{9,10},{10,1... | collective-permute-start | bytes 393224 | tf_op jit(solution)/shard_map/while/body/eval_jaxpr/ppermute | solution.py:13
  77.8 8.1 %collective-permute-start.1 = (bf16[2,128,2,128]{3,1,2,0:T(8,128)(2,1)S(1)}, bf16[2,128,2,128]{3,1,2,0:T(8,128)(2,1)S(1)}, u32[]{:S(2)}, u32[]{:S(2)}) collective-permute-start(bf16[2,128,2,128]{3,1,2,0:T(8,128)(2,1)S(1)} %copy.54), channel_id=1, source_target_pairs={{0,1},{1,2},{2,3},{3,4},{4,5},{5,6},{6,7},{7,0},{8,9},{9,10},{10,1... | collective-permute-start | bytes 393224 | tf_op jit(solution)/shard_map/while/body/eval_jaxpr/ppermute | solution.py:13
  80.1 11.9 %collective-permute-start.2 = (f32[2,128,2,128]{3,1,2,0:T(8,128)}, f32[2,128,2,128]{3,1,2,0:T(8,128)S(1)}, u32[]{:S(2)}, u32[]{:S(2)}) collective-permute-start(f32[2,128,2,128]{3,1,2,0:T(8,128)} %maximum_add_fusion.2), channel_id=1, source_target_pairs={{0,1},{1,2},{2,3},{3,4},{4,5},{5,6},{6,7},{7,0},{8,9},{9,10},{10,1... | collective-permute-start | bytes 786440 | tf_op jit(solution)/shard_map/while/body/eval_jaxpr/ppermute | solution.py:13
  92.0 8.9 %collective-permute-start.1 = (bf16[2,128,2,128]{3,1,2,0:T(8,128)(2,1)S(1)}, bf16[2,128,2,128]{3,1,2,0:T(8,128)(2,1)S(1)}, u32[]{:S(2)}, u32[]{:S(2)}) collective-permute-start(bf16[2,128,2,128]{3,1,2,0:T(8,128)(2,1)S(1)} %copy.54), channel_id=1, source_target_pairs={{0,1},{1,2},{2,3},{3,4},{4,5},{5,6},{6,7},{7,0},{8,9},{9,10},{10,1... | collective-permute-start | bytes 393224 | tf_op jit(solution)/shard_map/while/body/eval_jaxpr/ppermute | solution.py:13
  94.3 11.9 %collective-permute-start.2 = (f32[2,128,2,128]{3,1,2,0:T(8,128)}, f32[2,128,2,128]{3,1,2,0:T(8,128)S(1)}, u32[]{:S(2)}, u32[]{:S(2)}) collective-permute-start(f32[2,128,2,128]{3,1,2,0:T(8,128)} %maximum_add_fusion.2), channel_id=1, source_target_pairs={{0,1},{1,2},{2,3},{3,4},{4,5},{5,6},{6,7},{7,0},{8,9},{9,10},{10,1... | collective-permute-start | bytes 786440 | tf_op jit(solution)/shard_map/while/body/eval_jaxpr/ppermute | solution.py:13
  106.2 8.3 %collective-permute-start.1 = (bf16[2,128,2,128]{3,1,2,0:T(8,128)(2,1)S(1)}, bf16[2,128,2,128]{3,1,2,0:T(8,128)(2,1)S(1)}, u32[]{:S(2)}, u32[]{:S(2)}) collective-permute-start(bf16[2,128,2,128]{3,1,2,0:T(8,128)(2,1)S(1)} %copy.54), channel_id=1, source_target_pairs={{0,1},{1,2},{2,3},{3,4},{4,5},{5,6},{6,7},{7,0},{8,9},{9,10},{10,1... | collective-permute-start | bytes 393224 | tf_op jit(solution)/shard_map/while/body/eval_jaxpr/ppermute | solution.py:13
  108.5 11.2 %collective-permute-start.2 = (f32[2,128,2,128]{3,1,2,0:T(8,128)}, f32[2,128,2,128]{3,1,2,0:T(8,128)S(1)}, u32[]{:S(2)}, u32[]{:S(2)}) collective-permute-start(f32[2,128,2,128]{3,1,2,0:T(8,128)} %maximum_add_fusion.2), channel_id=1, source_target_pairs={{0,1},{1,2},{2,3},{3,4},{4,5},{5,6},{6,7},{7,0},{8,9},{9,10},{10,1... | collective-permute-start | bytes 786440 | tf_op jit(solution)/shard_map/while/body/eval_jaxpr/ppermute | solution.py:13
  119.7 8.4 %collective-permute-start.1 = (bf16[2,128,2,128]{3,1,2,0:T(8,128)(2,1)S(1)}, bf16[2,128,2,128]{3,1,2,0:T(8,128)(2,1)S(1)}, u32[]{:S(2)}, u32[]{:S(2)}) collective-permute-start(bf16[2,128,2,128]{3,1,2,0:T(8,128)(2,1)S(1)} %copy.54), channel_id=1, source_target_pairs={{0,1},{1,2},{2,3},{3,4},{4,5},{5,6},{6,7},{7,0},{8,9},{9,10},{10,1... | collective-permute-start | bytes 393224 | tf_op jit(solution)/shard_map/while/body/eval_jaxpr/ppermute | solution.py:13
  122.0 11.1 %collective-permute-start.2 = (f32[2,128,2,128]{3,1,2,0:T(8,128)}, f32[2,128,2,128]{3,1,2,0:T(8,128)S(1)}, u32[]{:S(2)}, u32[]{:S(2)}) collective-permute-start(f32[2,128,2,128]{3,1,2,0:T(8,128)} %maximum_add_fusion.2), channel_id=1, source_target_pairs={{0,1},{1,2},{2,3},{3,4},{4,5},{5,6},{6,7},{7,0},{8,9},{9,10},{10,1... | collective-permute-start | bytes 786440 | tf_op jit(solution)/shard_map/while/body/eval_jaxpr/ppermute | solution.py:13
  133.1 8.6 %collective-permute-start.1 = (bf16[2,128,2,128]{3,1,2,0:T(8,128)(2,1)S(1)}, bf16[2,128,2,128]{3,1,2,0:T(8,128)(2,1)S(1)}, u32[]{:S(2)}, u32[]{:S(2)}) collective-permute-start(bf16[2,128,2,128]{3,1,2,0:T(8,128)(2,1)S(1)} %copy.54), channel_id=1, source_target_pairs={{0,1},{1,2},{2,3},{3,4},{4,5},{5,6},{6,7},{7,0},{8,9},{9,10},{10,1... | collective-permute-start | bytes 393224 | tf_op jit(solution)/shard_map/while/body/eval_jaxpr/ppermute | solution.py:13
  135.3 11.1 %collective-permute-start.2 = (f32[2,128,2,128]{3,1,2,0:T(8,128)}, f32[2,128,2,128]{3,1,2,0:T(8,128)S(1)}, u32[]{:S(2)}, u32[]{:S(2)}) collective-permute-start(f32[2,128,2,128]{3,1,2,0:T(8,128)} %maximum_add_fusion.2), channel_id=1, source_target_pairs={{0,1},{1,2},{2,3},{3,4},{4,5},{5,6},{6,7},{7,0},{8,9},{9,10},{10,1... | collective-permute-start | bytes 786440 | tf_op jit(solution)/shard_map/while/body/eval_jaxpr/ppermute | solution.py:13
  146.4 8.6 %collective-permute-start.1 = (bf16[2,128,2,128]{3,1,2,0:T(8,128)(2,1)S(1)}, bf16[2,128,2,128]{3,1,2,0:T(8,128)(2,1)S(1)}, u32[]{:S(2)}, u32[]{:S(2)}) collective-permute-start(bf16[2,128,2,128]{3,1,2,0:T(8,128)(2,1)S(1)} %copy.54), channel_id=1, source_target_pairs={{0,1},{1,2},{2,3},{3,4},{4,5},{5,6},{6,7},{7,0},{8,9},{9,10},{10,1... | collective-permute-start | bytes 393224 | tf_op jit(solution)/shard_map/while/body/eval_jaxpr/ppermute | solution.py:13
  148.7 11.1 %collective-permute-start.2 = (f32[2,128,2,128]{3,1,2,0:T(8,128)}, f32[2,128,2,128]{3,1,2,0:T(8,128)S(1)}, u32[]{:S(2)}, u32[]{:S(2)}) collective-permute-start(f32[2,128,2,128]{3,1,2,0:T(8,128)} %maximum_add_fusion.2), channel_id=1, source_target_pairs={{0,1},{1,2},{2,3},{3,4},{4,5},{5,6},{6,7},{7,0},{8,9},{9,10},{10,1... | collective-permute-start | bytes 786440 | tf_op jit(solution)/shard_map/while/body/eval_jaxpr/ppermute | solution.py:13
  159.7 8.6 %collective-permute-start.1 = (bf16[2,128,2,128]{3,1,2,0:T(8,128)(2,1)S(1)}, bf16[2,128,2,128]{3,1,2,0:T(8,128)(2,1)S(1)}, u32[]{:S(2)}, u32[]{:S(2)}) collective-permute-start(bf16[2,128,2,128]{3,1,2,0:T(8,128)(2,1)S(1)} %copy.54), channel_id=1, source_target_pairs={{0,1},{1,2},{2,3},{3,4},{4,5},{5,6},{6,7},{7,0},{8,9},{9,10},{10,1... | collective-permute-start | bytes 393224 | tf_op jit(solution)/shard_map/while/body/eval_jaxpr/ppermute | solution.py:13
  162.0 11.1 %collective-permute-start.2 = (f32[2,128,2,128]{3,1,2,0:T(8,128)}, f32[2,128,2,128]{3,1,2,0:T(8,128)S(1)}, u32[]{:S(2)}, u32[]{:S(2)}) collective-permute-start(f32[2,128,2,128]{3,1,2,0:T(8,128)} %maximum_add_fusion.2), channel_id=1, source_target_pairs={{0,1},{1,2},{2,3},{3,4},{4,5},{5,6},{6,7},{7,0},{8,9},{9,10},{10,1... | collective-permute-start | bytes 786440 | tf_op jit(solution)/shard_map/while/body/eval_jaxpr/ppermute | solution.py:13
  173.1 7.7 %collective-permute-start.1 = (bf16[2,128,2,128]{3,1,2,0:T(8,128)(2,1)S(1)}, bf16[2,128,2,128]{3,1,2,0:T(8,128)(2,1)S(1)}, u32[]{:S(2)}, u32[]{:S(2)}) collective-permute-start(bf16[2,128,2,128]{3,1,2,0:T(8,128)(2,1)S(1)} %copy.54), channel_id=1, source_target_pairs={{0,1},{1,2},{2,3},{3,4},{4,5},{5,6},{6,7},{7,0},{8,9},{9,10},{10,1... | collective-permute-start | bytes 393224 | tf_op jit(solution)/shard_map/while/body/eval_jaxpr/ppermute | solution.py:13
  175.4 9.3 %collective-permute-start.2 = (f32[2,128,2,128]{3,1,2,0:T(8,128)}, f32[2,128,2,128]{3,1,2,0:T(8,128)S(1)}, u32[]{:S(2)}, u32[]{:S(2)}) collective-permute-start(f32[2,128,2,128]{3,1,2,0:T(8,128)} %maximum_add_fusion.2), channel_id=1, source_target_pairs={{0,1},{1,2},{2,3},{3,4},{4,5},{5,6},{6,7},{7,0},{8,9},{9,10},{10,1... | collective-permute-start | bytes 786440 | tf_op jit(solution)/shard_map/while/body/eval_jaxpr/ppermute | solution.py:13
  184.7 0.7 copy-start
Sparse Core Ops, SparseCore 0:
  185.5 31.2 all-reduce.1
where the time goes:
time: 226 us
  waiting for transfers between devices  171 us (76%)
  matrix products  19.9 us (9%)
  between operations  14.2 us (6%)
  local copies, waits for them, and re-layouts  8.24 us (4%)
  other arithmetic  7.6 us (3%)
  starting transfers between devices  3.98 us (2%)
    ppermute x24, waiting for transfers between devices, from_behind(): lax.ppermute(value, axis, [(i, (i + by) % peers) for i in range(peers)])  140 us
    psum x1, waiting for transfers between devices, local(): summed = lax.psum(grads_acc, 'pb')  30.3 us
    add x8, other arithmetic, grad_step(): grads_acc = grads_acc + jnp.stack([dk_part, dv_part])  5.9 us
    dot_general x16, matrix products, block_scores(): jnp.einsum('qhd,khd->hqk', query_blk, key_blk, preferred_element_type=jnp...  5.65 us
    dot_general x16, matrix products, block_scores(): jnp.einsum('qhd,khd->hqk', grad_blk, value_blk, preferred_element_type=jn...  5.56 us
    unnamed x15, local copies, waits for them, and re-layouts  5.08 us
  transfers between devices with their start and end apart: 25, of which 25 were waited for; matrix products, arithmetic and copies ran while one was open for 13% of the time, Pallas kernels for 0%

commit v1 on v0

--- a/solution.py
+++ b/solution.py
@@ -102,7 +102,7 @@
     )
     key_vals, grads_acc, dq_acc = lax.fori_loop(0, cycle_size, grad_step, start)
     dq = dq_acc.reshape(query_rows, H * DH)
-    summed = lax.psum(grads_acc, "pb")
+    summed = jnp.sum(lax.all_gather(grads_acc, "pb"), axis=0)
     return (dq, summed[0].reshape(key_rows, H * DH), summed[1].reshape(key_rows, H * DH))
 
 

time: 226 us -> 211 us (0.934)
  waiting for transfers between devices: 171 us -> 155 us
    psum x1 -> x0, waiting for transfers between devices: 30.3 us -> none  [local(): summed = lax.psum(grads_acc, 'pb')]
    all_gather x0 -> x1, waiting for transfers between devices: none -> 14.8 us  [local(): summed = jnp.sum(lax.all_gather(grads_acc, 'pb'), axis=0)]
    unnamed x15 -> x17, local copies, waits for them, and re-layouts: 5.08 us -> 6.59 us
where the time goes in v1:
time: 211 us
  waiting for transfers between devices  155 us (73%)
  matrix products  19.9 us (9%)
  between operations  14.2 us (7%)
  other arithmetic  8.84 us (4%)
  local copies, waits for them, and re-layouts  8.05 us (4%)
  starting transfers between devices  3.98 us (2%)
    ppermute x24, waiting for transfers between devices, from_behind(): lax.ppermute(value, axis, [(i, (i + by) % peers) for i in range(peers)])  141 us
    all_gather x1, waiting for transfers between devices, local(): summed = jnp.sum(lax.all_gather(grads_acc, 'pb'), axis=0)  14.8 us
    unnamed x17, local copies, waits for them, and re-layouts  6.59 us
    add x8, other arithmetic, grad_step(): grads_acc = grads_acc + jnp.stack([dk_part, dv_part])  5.86 us
    dot_general x16, matrix products, block_scores(): jnp.einsum('qhd,khd->hqk', query_blk, key_blk, preferred_element_type=jnp...  5.64 us
    dot_general x16, matrix products, block_scores(): jnp.einsum('qhd,khd->hqk', grad_blk, value_blk, preferred_element_type=jn...  5.47 us
  transfers between devices with their start and end apart: 25, of which 25 were waited for; matrix products, arithmetic and copies ran while one was open for 13% of the time, Pallas kernels for 0%

profile of v1, /device:TPU:0, one launch (start us, length us, event | category | flops | bytes accessed | tf_op | source)
XLA Modules:
  0.0 211.1 jit_solution(11502665543856636821)
XLA Ops:
  7.2 1.2 copy.38
  8.8 0.8 copy-done.1
  11.7 66.0 %while.32 = (s32[]{:T(128)}, bf16[2,128,2,128]{3,1,2,0:T(8,128)(2,1)S(1)}, f32[2,1024]{1,0:T(2,128)S(1)}, f32[2,1024]{1,0:T(2,128)S(1)}, f32[2,1024]{1,0:T(2,128...) while((s32[]{:T(128)}, ...), condition=%wide.region_4.0_spmd.clone, body=%wide.region_0.0_spmd.clone.sunk | while | flops 136067072 | bytes 5259408 | solution.py:84
  11.7 3.0 %collective-permute-start = (bf16[2,128,2,128]{3,1,2,0:T(8,128)(2,1)S(1)}, bf16[2,128,2,128]{3,1,2,0:T(8,128)(2,1)S(1)}, u32[]{:S(2)}, u32[]{:S(2)}) collective-permute-start(bf16[2,128,2,128]{3,1,2,0:T(8,128)(2,1)S(1)} %copy.60), channel_id=1, source_target_pairs={{0,1},{1,2},{2,3},{3,4},{4,5},{5,6},{6,7},{7,0},{8,9},{9,10},{10,1... | collective-permute-start | bytes 393224 | tf_op jit(solution)/shard_map/while/body/eval_jaxpr/ppermute | solution.py:13
  15.7 5.7 %collective-permute-done = bf16[2,128,2,128]{3,1,2,0:T(8,128)(2,1)S(1)} collective-permute-done((bf16[2,128,2,128]{3,1,2,0:T(8,128)(2,1)S(1)}, bf16[2,128,2,128]{3,1,2,0:T(8,128)(2,1)S(1)}, u32[]{:S(2)}, u32[]{:S(2)}) %collective-permute-start) | collective-permute-done | bytes 131104 | tf_op jit(solution)/shard_map/while/body/eval_jaxpr/ppermute | solution.py:13
  22.3 6.8 %collective-permute-done = bf16[2,128,2,128]{3,1,2,0:T(8,128)(2,1)S(1)} collective-permute-done((bf16[2,128,2,128]{3,1,2,0:T(8,128)(2,1)S(1)}, bf16[2,128,2,128]{3,1,2,0:T(8,128)(2,1)S(1)}, u32[]{:S(2)}, u32[]{:S(2)}) %collective-permute-start) | collective-permute-done | bytes 131104 | tf_op jit(solution)/shard_map/while/body/eval_jaxpr/ppermute | solution.py:13
  30.0 6.8 %collective-permute-done = bf16[2,128,2,128]{3,1,2,0:T(8,128)(2,1)S(1)} collective-permute-done((bf16[2,128,2,128]{3,1,2,0:T(8,128)(2,1)S(1)}, bf16[2,128,2,128]{3,1,2,0:T(8,128)(2,1)S(1)}, u32[]{:S(2)}, u32[]{:S(2)}) %collective-permute-start) | collective-permute-done | bytes 131104 | tf_op jit(solution)/shard_map/while/body/eval_jaxpr/ppermute | solution.py:13
  37.7 6.8 %collective-permute-done = bf16[2,128,2,128]{3,1,2,0:T(8,128)(2,1)S(1)} collective-permute-done((bf16[2,128,2,128]{3,1,2,0:T(8,128)(2,1)S(1)}, bf16[2,128,2,128]{3,1,2,0:T(8,128)(2,1)S(1)}, u32[]{:S(2)}, u32[]{:S(2)}) %collective-permute-start) | collective-permute-done | bytes 131104 | tf_op jit(solution)/shard_map/while/body/eval_jaxpr/ppermute | solution.py:13
  45.5 6.8 %collective-permute-done = bf16[2,128,2,128]{3,1,2,0:T(8,128)(2,1)S(1)} collective-permute-done((bf16[2,128,2,128]{3,1,2,0:T(8,128)(2,1)S(1)}, bf16[2,128,2,128]{3,1,2,0:T(8,128)(2,1)S(1)}, u32[]{:S(2)}, u32[]{:S(2)}) %collective-permute-start) | collective-permute-done | bytes 131104 | tf_op jit(solution)/shard_map/while/body/eval_jaxpr/ppermute | solution.py:13
  53.2 7.9 %collective-permute-done = bf16[2,128,2,128]{3,1,2,0:T(8,128)(2,1)S(1)} collective-permute-done((bf16[2,128,2,128]{3,1,2,0:T(8,128)(2,1)S(1)}, bf16[2,128,2,128]{3,1,2,0:T(8,128)(2,1)S(1)}, u32[]{:S(2)}, u32[]{:S(2)}) %collective-permute-start) | collective-permute-done | bytes 131104 | tf_op jit(solution)/shard_map/while/body/eval_jaxpr/ppermute | solution.py:13
  62.1 7.3 %collective-permute-done = bf16[2,128,2,128]{3,1,2,0:T(8,128)(2,1)S(1)} collective-permute-done((bf16[2,128,2,128]{3,1,2,0:T(8,128)(2,1)S(1)}, bf16[2,128,2,128]{3,1,2,0:T(8,128)(2,1)S(1)}, u32[]{:S(2)}, u32[]{:S(2)}) %collective-permute-start) | collective-permute-done | bytes 131104 | tf_op jit(solution)/shard_map/while/body/eval_jaxpr/ppermute | solution.py:13
  70.3 7.4 %collective-permute-done = bf16[2,128,2,128]{3,1,2,0:T(8,128)(2,1)S(1)} collective-permute-done((bf16[2,128,2,128]{3,1,2,0:T(8,128)(2,1)S(1)}, bf16[2,128,2,128]{3,1,2,0:T(8,128)(2,1)S(1)}, u32[]{:S(2)}, u32[]{:S(2)}) %collective-permute-start) | collective-permute-done | bytes 131104 | tf_op jit(solution)/shard_map/while/body/eval_jaxpr/ppermute | solution.py:13
  77.8 106.8 %while.33 = (s32[]{:T(128)}, bf16[2,128,2,128]{3,1,2,0:T(8,128)(2,1)S(1)}, f32[2,128,2,128]{3,1,2,0:T(8,128)S(1)}, f32[1024,2,128]{2,0,1:T(8,128)S(1)}, bf16[102...) while((s32[]{:T(128)}, ...), condition=%wide.region_6.0_spmd.clone, body=%wide.region_5.0_spmd.clone.sunk | while | flops 338067456 | bytes 12009663 | solution.py:103
  80.5 5.5 %collective-permute-done.1 = bf16[2,128,2,128]{3,1,2,0:T(8,128)(2,1)S(1)} collective-permute-done((bf16[2,128,2,128]{3,1,2,0:T(8,128)(2,1)S(1)}, bf16[2,128,2,128]{3,1,2,0:T(8,128)(2,1)S(1)}, u32[]{:S(2)}, u32[]{:S(2)}) %collective-permute-start.1) | collective-permute-done | bytes 131104 | tf_op jit(solution)/shard_map/while/body/eval_jaxpr/ppermute | solution.py:13
  86.0 6.0 %collective-permute-done.2 = f32[2,128,2,128]{3,1,2,0:T(8,128)S(1)} collective-permute-done((f32[2,128,2,128]{3,1,2,0:T(8,128)}, f32[2,128,2,128]{3,1,2,0:T(8,128)S(1)}, u32[]{:S(2)}, u32[]{:S(2)}) %collective-permute-start.2) | collective-permute-done | bytes 262176 | tf_op jit(solution)/shard_map/while/body/eval_jaxpr/ppermute | solution.py:13
  94.7 6.2 %collective-permute-done.1 = bf16[2,128,2,128]{3,1,2,0:T(8,128)(2,1)S(1)} collective-permute-done((bf16[2,128,2,128]{3,1,2,0:T(8,128)(2,1)S(1)}, bf16[2,128,2,128]{3,1,2,0:T(8,128)(2,1)S(1)}, u32[]{:S(2)}, u32[]{:S(2)}) %collective-permute-start.1) | collective-permute-done | bytes 131104 | tf_op jit(solution)/shard_map/while/body/eval_jaxpr/ppermute | solution.py:13
  100.9 5.2 %collective-permute-done.2 = f32[2,128,2,128]{3,1,2,0:T(8,128)S(1)} collective-permute-done((f32[2,128,2,128]{3,1,2,0:T(8,128)}, f32[2,128,2,128]{3,1,2,0:T(8,128)S(1)}, u32[]{:S(2)}, u32[]{:S(2)}) %collective-permute-start.2) | collective-permute-done | bytes 262176 | tf_op jit(solution)/shard_map/while/body/eval_jaxpr/ppermute | solution.py:13
  108.9 5.6 %collective-permute-done.1 = bf16[2,128,2,128]{3,1,2,0:T(8,128)(2,1)S(1)} collective-permute-done((bf16[2,128,2,128]{3,1,2,0:T(8,128)(2,1)S(1)}, bf16[2,128,2,128]{3,1,2,0:T(8,128)(2,1)S(1)}, u32[]{:S(2)}, u32[]{:S(2)}) %collective-permute-start.1) | collective-permute-done | bytes 131104 | tf_op jit(solution)/shard_map/while/body/eval_jaxpr/ppermute | solution.py:13
  114.5 5.2 %collective-permute-done.2 = f32[2,128,2,128]{3,1,2,0:T(8,128)S(1)} collective-permute-done((f32[2,128,2,128]{3,1,2,0:T(8,128)}, f32[2,128,2,128]{3,1,2,0:T(8,128)S(1)}, u32[]{:S(2)}, u32[]{:S(2)}) %collective-permute-start.2) | collective-permute-done | bytes 262176 | tf_op jit(solution)/shard_map/while/body/eval_jaxpr/ppermute | solution.py:13
  122.4 5.7 %collective-permute-done.1 = bf16[2,128,2,128]{3,1,2,0:T(8,128)(2,1)S(1)} collective-permute-done((bf16[2,128,2,128]{3,1,2,0:T(8,128)(2,1)S(1)}, bf16[2,128,2,128]{3,1,2,0:T(8,128)(2,1)S(1)}, u32[]{:S(2)}, u32[]{:S(2)}) %collective-permute-start.1) | collective-permute-done | bytes 131104 | tf_op jit(solution)/shard_map/while/body/eval_jaxpr/ppermute | solution.py:13
  128.1 4.9 %collective-permute-done.2 = f32[2,128,2,128]{3,1,2,0:T(8,128)S(1)} collective-permute-done((f32[2,128,2,128]{3,1,2,0:T(8,128)}, f32[2,128,2,128]{3,1,2,0:T(8,128)S(1)}, u32[]{:S(2)}, u32[]{:S(2)}) %collective-permute-start.2) | collective-permute-done | bytes 262176 | tf_op jit(solution)/shard_map/while/body/eval_jaxpr/ppermute | solution.py:13
  135.7 5.9 %collective-permute-done.1 = bf16[2,128,2,128]{3,1,2,0:T(8,128)(2,1)S(1)} collective-permute-done((bf16[2,128,2,128]{3,1,2,0:T(8,128)(2,1)S(1)}, bf16[2,128,2,128]{3,1,2,0:T(8,128)(2,1)S(1)}, u32[]{:S(2)}, u32[]{:S(2)}) %collective-permute-start.1) | collective-permute-done | bytes 131104 | tf_op jit(solution)/shard_map/while/body/eval_jaxpr/ppermute | solution.py:13
  141.6 4.8 %collective-permute-done.2 = f32[2,128,2,128]{3,1,2,0:T(8,128)S(1)} collective-permute-done((f32[2,128,2,128]{3,1,2,0:T(8,128)}, f32[2,128,2,128]{3,1,2,0:T(8,128)S(1)}, u32[]{:S(2)}, u32[]{:S(2)}) %collective-permute-start.2) | collective-permute-done | bytes 262176 | tf_op jit(solution)/shard_map/while/body/eval_jaxpr/ppermute | solution.py:13
  149.1 5.9 %collective-permute-done.1 = bf16[2,128,2,128]{3,1,2,0:T(8,128)(2,1)S(1)} collective-permute-done((bf16[2,128,2,128]{3,1,2,0:T(8,128)(2,1)S(1)}, bf16[2,128,2,128]{3,1,2,0:T(8,128)(2,1)S(1)}, u32[]{:S(2)}, u32[]{:S(2)}) %collective-permute-start.1) | collective-permute-done | bytes 131104 | tf_op jit(solution)/shard_map/while/body/eval_jaxpr/ppermute | solution.py:13
  155.0 4.8 %collective-permute-done.2 = f32[2,128,2,128]{3,1,2,0:T(8,128)S(1)} collective-permute-done((f32[2,128,2,128]{3,1,2,0:T(8,128)}, f32[2,128,2,128]{3,1,2,0:T(8,128)S(1)}, u32[]{:S(2)}, u32[]{:S(2)}) %collective-permute-start.2) | collective-permute-done | bytes 262176 | tf_op jit(solution)/shard_map/while/body/eval_jaxpr/ppermute | solution.py:13
  162.4 5.9 %collective-permute-done.1 = bf16[2,128,2,128]{3,1,2,0:T(8,128)(2,1)S(1)} collective-permute-done((bf16[2,128,2,128]{3,1,2,0:T(8,128)(2,1)S(1)}, bf16[2,128,2,128]{3,1,2,0:T(8,128)(2,1)S(1)}, u32[]{:S(2)}, u32[]{:S(2)}) %collective-permute-start.1) | collective-permute-done | bytes 131104 | tf_op jit(solution)/shard_map/while/body/eval_jaxpr/ppermute | solution.py:13
  168.3 4.8 %collective-permute-done.2 = f32[2,128,2,128]{3,1,2,0:T(8,128)S(1)} collective-permute-done((f32[2,128,2,128]{3,1,2,0:T(8,128)}, f32[2,128,2,128]{3,1,2,0:T(8,128)S(1)}, u32[]{:S(2)}, u32[]{:S(2)}) %collective-permute-start.2) | collective-permute-done | bytes 262176 | tf_op jit(solution)/shard_map/while/body/eval_jaxpr/ppermute | solution.py:13
  175.8 5.0 %collective-permute-done.1 = bf16[2,128,2,128]{3,1,2,0:T(8,128)(2,1)S(1)} collective-permute-done((bf16[2,128,2,128]{3,1,2,0:T(8,128)(2,1)S(1)}, bf16[2,128,2,128]{3,1,2,0:T(8,128)(2,1)S(1)}, u32[]{:S(2)}, u32[]{:S(2)}) %collective-permute-start.1) | collective-permute-done | bytes 131104 | tf_op jit(solution)/shard_map/while/body/eval_jaxpr/ppermute | solution.py:13
  180.8 3.8 %collective-permute-done.2 = f32[2,128,2,128]{3,1,2,0:T(8,128)S(1)} collective-permute-done((f32[2,128,2,128]{3,1,2,0:T(8,128)}, f32[2,128,2,128]{3,1,2,0:T(8,128)S(1)}, u32[]{:S(2)}, u32[]{:S(2)}) %collective-permute-start.2) | collective-permute-done | bytes 262176 | tf_op jit(solution)/shard_map/while/body/eval_jaxpr/ppermute | solution.py:13
  185.4 1.1 copy_bitcast_fusion
  186.4 14.8 %all-gather.3.cloned.1.call-done = f32[8,128,2,128]{3,1,2,0:T(8,128)} async-done(((f32[2,128,2,128]{3,1,2,0:T(8,128)}), f32[8,128,2,128]{3,1,2,0:T(8,128)}) %all-gather.3.cloned.1.call-update) | async-done | bytes 1048592 | tf_op jit(solution)/shard_map/all_gather | solution.py:105
  201.2 1.3 reduce_sum.27
  (162 shorter events, 33.4 us)
Async XLA Ops:
  7.2 194.0 %all-gather.3.cloned.1.call-start = ((), (), s32[]{:S(2)}) async-start(), calls=%async_computation | async-start | bytes 1310720 | tf_op jit(solution)/shard_map/all_gather | solution.py:105
  8.5 1.0 copy-start.1
  9.8 0.8 copy-start.2
  10.6 0.8 copy-start.3
  11.7 9.6 %collective-permute-start = (bf16[2,128,2,128]{3,1,2,0:T(8,128)(2,1)S(1)}, bf16[2,128,2,128]{3,1,2,0:T(8,128)(2,1)S(1)}, u32[]{:S(2)}, u32[]{:S(2)}) collective-permute-start(bf16[2,128,2,128]{3,1,2,0:T(8,128)(2,1)S(1)} %copy.60), channel_id=1, source_target_pairs={{0,1},{1,2},{2,3},{3,4},{4,5},{5,6},{6,7},{7,0},{8,9},{9,10},{10,1... | collective-permute-start | bytes 393224 | tf_op jit(solution)/shard_map/while/body/eval_jaxpr/ppermute | solution.py:13
  21.3 7.7 %collective-permute-start = (bf16[2,128,2,128]{3,1,2,0:T(8,128)(2,1)S(1)}, bf16[2,128,2,128]{3,1,2,0:T(8,128)(2,1)S(1)}, u32[]{:S(2)}, u32[]{:S(2)}) collective-permute-start(bf16[2,128,2,128]{3,1,2,0:T(8,128)(2,1)S(1)} %copy.60), channel_id=1, source_target_pairs={{0,1},{1,2},{2,3},{3,4},{4,5},{5,6},{6,7},{7,0},{8,9},{9,10},{10,1... | collective-permute-start | bytes 393224 | tf_op jit(solution)/shard_map/while/body/eval_jaxpr/ppermute | solution.py:13
  29.1 7.7 %collective-permute-start = (bf16[2,128,2,128]{3,1,2,0:T(8,128)(2,1)S(1)}, bf16[2,128,2,128]{3,1,2,0:T(8,128)(2,1)S(1)}, u32[]{:S(2)}, u32[]{:S(2)}) collective-permute-start(bf16[2,128,2,128]{3,1,2,0:T(8,128)(2,1)S(1)} %copy.60), channel_id=1, source_target_pairs={{0,1},{1,2},{2,3},{3,4},{4,5},{5,6},{6,7},{7,0},{8,9},{9,10},{10,1... | collective-permute-start | bytes 393224 | tf_op jit(solution)/shard_map/while/body/eval_jaxpr/ppermute | solution.py:13
  36.8 7.7 %collective-permute-start = (bf16[2,128,2,128]{3,1,2,0:T(8,128)(2,1)S(1)}, bf16[2,128,2,128]{3,1,2,0:T(8,128)(2,1)S(1)}, u32[]{:S(2)}, u32[]{:S(2)}) collective-permute-start(bf16[2,128,2,128]{3,1,2,0:T(8,128)(2,1)S(1)} %copy.60), channel_id=1, source_target_pairs={{0,1},{1,2},{2,3},{3,4},{4,5},{5,6},{6,7},{7,0},{8,9},{9,10},{10,1... | collective-permute-start | bytes 393224 | tf_op jit(solution)/shard_map/while/body/eval_jaxpr/ppermute | solution.py:13
  44.5 7.7 %collective-permute-start = (bf16[2,128,2,128]{3,1,2,0:T(8,128)(2,1)S(1)}, bf16[2,128,2,128]{3,1,2,0:T(8,128)(2,1)S(1)}, u32[]{:S(2)}, u32[]{:S(2)}) collective-permute-start(bf16[2,128,2,128]{3,1,2,0:T(8,128)(2,1)S(1)} %copy.60), channel_id=1, source_target_pairs={{0,1},{1,2},{2,3},{3,4},{4,5},{5,6},{6,7},{7,0},{8,9},{9,10},{10,1... | collective-permute-start | bytes 393224 | tf_op jit(solution)/shard_map/while/body/eval_jaxpr/ppermute | solution.py:13
  52.3 8.8 %collective-permute-start = (bf16[2,128,2,128]{3,1,2,0:T(8,128)(2,1)S(1)}, bf16[2,128,2,128]{3,1,2,0:T(8,128)(2,1)S(1)}, u32[]{:S(2)}, u32[]{:S(2)}) collective-permute-start(bf16[2,128,2,128]{3,1,2,0:T(8,128)(2,1)S(1)} %copy.60), channel_id=1, source_target_pairs={{0,1},{1,2},{2,3},{3,4},{4,5},{5,6},{6,7},{7,0},{8,9},{9,10},{10,1... | collective-permute-start | bytes 393224 | tf_op jit(solution)/shard_map/while/body/eval_jaxpr/ppermute | solution.py:13
  61.1 8.3 %collective-permute-start = (bf16[2,128,2,128]{3,1,2,0:T(8,128)(2,1)S(1)}, bf16[2,128,2,128]{3,1,2,0:T(8,128)(2,1)S(1)}, u32[]{:S(2)}, u32[]{:S(2)}) collective-permute-start(bf16[2,128,2,128]{3,1,2,0:T(8,128)(2,1)S(1)} %copy.60), channel_id=1, source_target_pairs={{0,1},{1,2},{2,3},{3,4},{4,5},{5,6},{6,7},{7,0},{8,9},{9,10},{10,1... | collective-permute-start | bytes 393224 | tf_op jit(solution)/shard_map/while/body/eval_jaxpr/ppermute | solution.py:13
  69.4 8.3 %collective-permute-start = (bf16[2,128,2,128]{3,1,2,0:T(8,128)(2,1)S(1)}, bf16[2,128,2,128]{3,1,2,0:T(8,128)(2,1)S(1)}, u32[]{:S(2)}, u32[]{:S(2)}) collective-permute-start(bf16[2,128,2,128]{3,1,2,0:T(8,128)(2,1)S(1)} %copy.60), channel_id=1, source_target_pairs={{0,1},{1,2},{2,3},{3,4},{4,5},{5,6},{6,7},{7,0},{8,9},{9,10},{10,1... | collective-permute-start | bytes 393224 | tf_op jit(solution)/shard_map/while/body/eval_jaxpr/ppermute | solution.py:13
  77.8 8.2 %collective-permute-start.1 = (bf16[2,128,2,128]{3,1,2,0:T(8,128)(2,1)S(1)}, bf16[2,128,2,128]{3,1,2,0:T(8,128)(2,1)S(1)}, u32[]{:S(2)}, u32[]{:S(2)}) collective-permute-start(bf16[2,128,2,128]{3,1,2,0:T(8,128)(2,1)S(1)} %copy.74), channel_id=1, source_target_pairs={{0,1},{1,2},{2,3},{3,4},{4,5},{5,6},{6,7},{7,0},{8,9},{9,10},{10,1... | collective-permute-start | bytes 393224 | tf_op jit(solution)/shard_map/while/body/eval_jaxpr/ppermute | solution.py:13
  80.1 11.9 %collective-permute-start.2 = (f32[2,128,2,128]{3,1,2,0:T(8,128)}, f32[2,128,2,128]{3,1,2,0:T(8,128)S(1)}, u32[]{:S(2)}, u32[]{:S(2)}) collective-permute-start(f32[2,128,2,128]{3,1,2,0:T(8,128)} %maximum_add_fusion.2), channel_id=1, source_target_pairs={{0,1},{1,2},{2,3},{3,4},{4,5},{5,6},{6,7},{7,0},{8,9},{9,10},{10,1... | collective-permute-start | bytes 786440 | tf_op jit(solution)/shard_map/while/body/eval_jaxpr/ppermute | solution.py:13
  92.0 8.9 %collective-permute-start.1 = (bf16[2,128,2,128]{3,1,2,0:T(8,128)(2,1)S(1)}, bf16[2,128,2,128]{3,1,2,0:T(8,128)(2,1)S(1)}, u32[]{:S(2)}, u32[]{:S(2)}) collective-permute-start(bf16[2,128,2,128]{3,1,2,0:T(8,128)(2,1)S(1)} %copy.74), channel_id=1, source_target_pairs={{0,1},{1,2},{2,3},{3,4},{4,5},{5,6},{6,7},{7,0},{8,9},{9,10},{10,1... | collective-permute-start | bytes 393224 | tf_op jit(solution)/shard_map/while/body/eval_jaxpr/ppermute | solution.py:13
  94.3 11.9 %collective-permute-start.2 = (f32[2,128,2,128]{3,1,2,0:T(8,128)}, f32[2,128,2,128]{3,1,2,0:T(8,128)S(1)}, u32[]{:S(2)}, u32[]{:S(2)}) collective-permute-start(f32[2,128,2,128]{3,1,2,0:T(8,128)} %maximum_add_fusion.2), channel_id=1, source_target_pairs={{0,1},{1,2},{2,3},{3,4},{4,5},{5,6},{6,7},{7,0},{8,9},{9,10},{10,1... | collective-permute-start | bytes 786440 | tf_op jit(solution)/shard_map/while/body/eval_jaxpr/ppermute | solution.py:13
  106.2 8.3 %collective-permute-start.1 = (bf16[2,128,2,128]{3,1,2,0:T(8,128)(2,1)S(1)}, bf16[2,128,2,128]{3,1,2,0:T(8,128)(2,1)S(1)}, u32[]{:S(2)}, u32[]{:S(2)}) collective-permute-start(bf16[2,128,2,128]{3,1,2,0:T(8,128)(2,1)S(1)} %copy.74), channel_id=1, source_target_pairs={{0,1},{1,2},{2,3},{3,4},{4,5},{5,6},{6,7},{7,0},{8,9},{9,10},{10,1... | collective-permute-start | bytes 393224 | tf_op jit(solution)/shard_map/while/body/eval_jaxpr/ppermute | solution.py:13
  108.4 11.2 %collective-permute-start.2 = (f32[2,128,2,128]{3,1,2,0:T(8,128)}, f32[2,128,2,128]{3,1,2,0:T(8,128)S(1)}, u32[]{:S(2)}, u32[]{:S(2)}) collective-permute-start(f32[2,128,2,128]{3,1,2,0:T(8,128)} %maximum_add_fusion.2), channel_id=1, source_target_pairs={{0,1},{1,2},{2,3},{3,4},{4,5},{5,6},{6,7},{7,0},{8,9},{9,10},{10,1... | collective-permute-start | bytes 786440 | tf_op jit(solution)/shard_map/while/body/eval_jaxpr/ppermute | solution.py:13
  119.7 8.4 %collective-permute-start.1 = (bf16[2,128,2,128]{3,1,2,0:T(8,128)(2,1)S(1)}, bf16[2,128,2,128]{3,1,2,0:T(8,128)(2,1)S(1)}, u32[]{:S(2)}, u32[]{:S(2)}) collective-permute-start(bf16[2,128,2,128]{3,1,2,0:T(8,128)(2,1)S(1)} %copy.74), channel_id=1, source_target_pairs={{0,1},{1,2},{2,3},{3,4},{4,5},{5,6},{6,7},{7,0},{8,9},{9,10},{10,1... | collective-permute-start | bytes 393224 | tf_op jit(solution)/shard_map/while/body/eval_jaxpr/ppermute | solution.py:13
  122.0 11.1 %collective-permute-start.2 = (f32[2,128,2,128]{3,1,2,0:T(8,128)}, f32[2,128,2,128]{3,1,2,0:T(8,128)S(1)}, u32[]{:S(2)}, u32[]{:S(2)}) collective-permute-start(f32[2,128,2,128]{3,1,2,0:T(8,128)} %maximum_add_fusion.2), channel_id=1, source_target_pairs={{0,1},{1,2},{2,3},{3,4},{4,5},{5,6},{6,7},{7,0},{8,9},{9,10},{10,1... | collective-permute-start | bytes 786440 | tf_op jit(solution)/shard_map/while/body/eval_jaxpr/ppermute | solution.py:13
  133.0 8.6 %collective-permute-start.1 = (bf16[2,128,2,128]{3,1,2,0:T(8,128)(2,1)S(1)}, bf16[2,128,2,128]{3,1,2,0:T(8,128)(2,1)S(1)}, u32[]{:S(2)}, u32[]{:S(2)}) collective-permute-start(bf16[2,128,2,128]{3,1,2,0:T(8,128)(2,1)S(1)} %copy.74), channel_id=1, source_target_pairs={{0,1},{1,2},{2,3},{3,4},{4,5},{5,6},{6,7},{7,0},{8,9},{9,10},{10,1... | collective-permute-start | bytes 393224 | tf_op jit(solution)/shard_map/while/body/eval_jaxpr/ppermute | solution.py:13
  135.3 11.1 %collective-permute-start.2 = (f32[2,128,2,128]{3,1,2,0:T(8,128)}, f32[2,128,2,128]{3,1,2,0:T(8,128)S(1)}, u32[]{:S(2)}, u32[]{:S(2)}) collective-permute-start(f32[2,128,2,128]{3,1,2,0:T(8,128)} %maximum_add_fusion.2), channel_id=1, source_target_pairs={{0,1},{1,2},{2,3},{3,4},{4,5},{5,6},{6,7},{7,0},{8,9},{9,10},{10,1... | collective-permute-start | bytes 786440 | tf_op jit(solution)/shard_map/while/body/eval_jaxpr/ppermute | solution.py:13
  146.4 8.6 %collective-permute-start.1 = (bf16[2,128,2,128]{3,1,2,0:T(8,128)(2,1)S(1)}, bf16[2,128,2,128]{3,1,2,0:T(8,128)(2,1)S(1)}, u32[]{:S(2)}, u32[]{:S(2)}) collective-permute-start(bf16[2,128,2,128]{3,1,2,0:T(8,128)(2,1)S(1)} %copy.74), channel_id=1, source_target_pairs={{0,1},{1,2},{2,3},{3,4},{4,5},{5,6},{6,7},{7,0},{8,9},{9,10},{10,1... | collective-permute-start | bytes 393224 | tf_op jit(solution)/shard_map/while/body/eval_jaxpr/ppermute | solution.py:13
  148.7 11.1 %collective-permute-start.2 = (f32[2,128,2,128]{3,1,2,0:T(8,128)}, f32[2,128,2,128]{3,1,2,0:T(8,128)S(1)}, u32[]{:S(2)}, u32[]{:S(2)}) collective-permute-start(f32[2,128,2,128]{3,1,2,0:T(8,128)} %maximum_add_fusion.2), channel_id=1, source_target_pairs={{0,1},{1,2},{2,3},{3,4},{4,5},{5,6},{6,7},{7,0},{8,9},{9,10},{10,1... | collective-permute-start | bytes 786440 | tf_op jit(solution)/shard_map/while/body/eval_jaxpr/ppermute | solution.py:13
  159.7 8.6 %collective-permute-start.1 = (bf16[2,128,2,128]{3,1,2,0:T(8,128)(2,1)S(1)}, bf16[2,128,2,128]{3,1,2,0:T(8,128)(2,1)S(1)}, u32[]{:S(2)}, u32[]{:S(2)}) collective-permute-start(bf16[2,128,2,128]{3,1,2,0:T(8,128)(2,1)S(1)} %copy.74), channel_id=1, source_target_pairs={{0,1},{1,2},{2,3},{3,4},{4,5},{5,6},{6,7},{7,0},{8,9},{9,10},{10,1... | collective-permute-start | bytes 393224 | tf_op jit(solution)/shard_map/while/body/eval_jaxpr/ppermute | solution.py:13
  162.0 11.1 %collective-permute-start.2 = (f32[2,128,2,128]{3,1,2,0:T(8,128)}, f32[2,128,2,128]{3,1,2,0:T(8,128)S(1)}, u32[]{:S(2)}, u32[]{:S(2)}) collective-permute-start(f32[2,128,2,128]{3,1,2,0:T(8,128)} %maximum_add_fusion.2), channel_id=1, source_target_pairs={{0,1},{1,2},{2,3},{3,4},{4,5},{5,6},{6,7},{7,0},{8,9},{9,10},{10,1... | collective-permute-start | bytes 786440 | tf_op jit(solution)/shard_map/while/body/eval_jaxpr/ppermute | solution.py:13
  173.1 7.7 %collective-permute-start.1 = (bf16[2,128,2,128]{3,1,2,0:T(8,128)(2,1)S(1)}, bf16[2,128,2,128]{3,1,2,0:T(8,128)(2,1)S(1)}, u32[]{:S(2)}, u32[]{:S(2)}) collective-permute-start(bf16[2,128,2,128]{3,1,2,0:T(8,128)(2,1)S(1)} %copy.74), channel_id=1, source_target_pairs={{0,1},{1,2},{2,3},{3,4},{4,5},{5,6},{6,7},{7,0},{8,9},{9,10},{10,1... | collective-permute-start | bytes 393224 | tf_op jit(solution)/shard_map/while/body/eval_jaxpr/ppermute | solution.py:13
  175.4 9.3 %collective-permute-start.2 = (f32[2,128,2,128]{3,1,2,0:T(8,128)}, f32[2,128,2,128]{3,1,2,0:T(8,128)S(1)}, u32[]{:S(2)}, u32[]{:S(2)}) collective-permute-start(f32[2,128,2,128]{3,1,2,0:T(8,128)} %maximum_add_fusion.2), channel_id=1, source_target_pairs={{0,1},{1,2},{2,3},{3,4},{4,5},{5,6},{6,7},{7,0},{8,9},{9,10},{10,1... | collective-permute-start | bytes 786440 | tf_op jit(solution)/shard_map/while/body/eval_jaxpr/ppermute | solution.py:13
  184.6 0.7 copy-start
Sparse Core Ops, SparseCore 0:
  185.5 15.6 all-gather.2
